TPU v7x, 32 devices: a whole 2x2x4 slice. The times are simulated.
32 devices in a mesh: group: 8 (over y, x, core), section: 4 (over z).
Axes of the slice: x: 2, y: 2, z: 4, core: 2. Of those that a mesh axis runs over, the one named last changes fastest.
Arguments:
- columns: float32 [8, 8, 16, 8192], P('group', None, None, 'section'), may hold values from -6 to 6
- vectors: bfloat16 [8, 8, 128, 8192], P('group', None, None, 'section'), may hold values from -0.0625 to 0.0625
- factors: float32 [8, 8, 128, 128], P('group'), as said below
- order: int32 [8], P('group'), may hold values from 4096 to 8192
- blocks: int32 [8], P('group'), may hold values from 1 to 8
- live: int32 [8, 8], P('group'), may hold values from 0 to 16
Outputs:
- result: float32 [8, 8, 16, 8192], P('group', None, None, 'section')
Inputs may be any that keep to these rules, and one draw needn't show every extreme that they name: `factors`: upper triangular, diagonal entries between one half and two, off-diagonal entries small.
All inputs are finite; a program needn't handle non-finite values.
Results may differ from a plain program's by a relative error of at most 0.0003.
Values sent between devices are 32-bit elements; how exact they have to be, the bound alone decides.
No kernel may reach another device: no remote copies, remote signals or barrier semaphores. Data moves between devices by JAX's collectives and lax.ppermute only.
A program may use at most 64 MiB of HBM per device.

v0:
```python
import jax
import jax.numpy as jnp
from jax import lax
from jax.sharding import PartitionSpec as P


def shards(columns, vectors, factors, order, blocks, live):
    count = vectors.shape[1]
    width = vectors.shape[2]
    rows = vectors.shape[3]
    slots = columns.shape[2]
    first_row = lax.axis_index("section") * rows
    inside = (first_row + jnp.arange(rows) < order[0]).astype(jnp.float32)
    basis_all = vectors[0].astype(jnp.float32) * inside[None, None, :]
    active = (jnp.arange(count) < blocks[0]).astype(jnp.float32)
    factor_all = factors[0] * active[:, None, None]
    high = lax.Precision.HIGHEST
    local_correlation = jnp.einsum("jar,jbr->jab", basis_all[0::2], basis_all[1::2], precision=high)
    correlation_all = lax.psum(local_correlation, "section")
    merged = []
    zeros = jnp.zeros((width, width), jnp.float32)
    for pair in range(count // 2):
        upper_t = factor_all[2 * pair]
        lower_t = factor_all[2 * pair + 1]
        corner = -jnp.dot(
            jnp.dot(upper_t, correlation_all[pair], precision=high), lower_t, precision=high
        )
        top = jnp.concatenate([upper_t, corner], axis=1)
        bottom = jnp.concatenate([zeros, lower_t], axis=1)
        joined = jnp.concatenate([basis_all[2 * pair], basis_all[2 * pair + 1]], axis=0)
        merged.append((joined, jnp.concatenate([top, bottom], axis=0)))
    held = lax.all_to_all(columns[0], "group", split_axis=0, concat_axis=0, tiled=True)
    shape = held.shape
    panel = held.reshape(shape[0] * shape[1], shape[2])
    transform_panel = panel
    for pair in reversed(range(count // 2)):
        joined, factor = merged[pair]
        inner = lax.psum(jnp.dot(transform_panel, joined.T, precision=high), "section")
        scaled = jnp.dot(inner, factor.T, precision=high)
        transform_panel = transform_panel - jnp.dot(scaled, joined, precision=high)
    moved = transform_panel.reshape(shape)
    returned = lax.all_to_all(moved, "group", split_axis=0, concat_axis=0, tiled=True)
    keep = jnp.arange(slots)[None, :] < live[0][:, None]
    return jnp.where(keep[:, :, None], returned, jnp.float32(0.0))[None]


def solution(mesh):
    return jax.shard_map(
        shards,
        mesh=mesh,
        in_specs=(
            P("group", None, None, "section"),
            P("group", None, None, "section"),
            P("group", None, None, None),
            P("group"),
            P("group"),
            P("group", None),
        ),
        out_specs=P("group", None, None, "section"),
        check_vma=False,
    )
```

profile of v0, /device:TPU:0, one launch (start us, length us, event | category | flops | bytes accessed | tf_op | source)
XLA Modules:
  0.0 233.6 jit_solution(4334425276789696389)
XLA Ops:
  6.5 5.2 %all-to-all-start = ((f32[8,16,2048]{2,1,0:T(8,128)}), f32[8,16,2048]{2,1,0:T(8,128)}, u32[]{:S(2)}, u32[]{:S(2)}) async-start(f32[8,16,2048]{2,1,0:T(8,128)} %bitcast.85), calls=%async_computation | async-start | bytes 2097152 | tf_op jit(solution)/shard_map/all_to_all | solution.py:32
  12.4 3.4 %convert_multiply_fusion = f32[8,128,2048]{2,1,0:T(8,128)S(1)} fusion(bf16[1,8,128,2048]{3,2,1,0:T(8,128)(2,1)} %param.7, f32[2048]{0:T(1024)S(1)} %fusion.40), kind=kLoop, calls=%fused_computation | loop fusion | flops 4194304 | bytes 12591104 | tf_op jit(solution)/shard_map/mul | solution.py:14
  15.8 4.7 %fusion = f32[4,128,128]{2,1,0:T(8,128)} fusion(f32[8,128,2048]{2,1,0:T(8,128)S(1)} %convert_multiply_fusion), kind=kOutput, calls=%fused_computation.1 | convolution fusion | flops 1610612736 | bytes 8650752 | tf_op jit(solution)/shard_map/jar,jbr->jab/dot_general | solution.py:18
  21.1 2.5 %slice_bitcast_fusion.1 = (f32[128,2048]{1,0:T(8,128)S(1)}, f32[128,2048]{1,0:T(8,128)S(1)}, f32[128,2048]{1,0:T(8,128)}, f32[128,2048]{1,0:T(8,128)}, f32[128,2...) fusion(f32[8,128,2048]{2,1,0:T(8,128)S(1)} %convert_multiply_fusion), kind=kLoop, calls=%fused_computation.22 | loop fusion | bytes 16777216 | tf_op jit(solution)/shard_map/squeeze | solution.py:30
  23.6 3.6 %all-to-all-done = f32[8,16,2048]{2,1,0:T(8,128)} async-done(((f32[8,16,2048]{2,1,0:T(8,128)}), f32[8,16,2048]{2,1,0:T(8,128)}, u32[]{:S(2)}, u32[]{:S(2)}) %all-to-all-start) | async-done | bytes 1048608 | tf_op jit(solution)/shard_map/all_to_all | solution.py:32
  27.2 4.3 %fusion.7 = f32[128,256]{0,1:T(8,128)} fusion(f32[128,2048]{1,0:T(8,128)} %bitcast.2, f32[128,2048]{1,0:T(8,128)} %get-tuple-element.13, f32[128,2048]{1,0:T(8,128)} %get-tuple-element.14), kind=kOutput, calls=%fused_computation.16 | convolution fusion | flops 805830656 | bytes 3276800 | tf_op jit(solution)/shard_map/dot_general | solution.py:38
  31.6 1.1 bitcast_multiply_fusion
  34.3 34.2 %all-reduce.16.cloned.1.call-done = (f32[128,256]{0,1:T(8,128)}, f32[4,128,128]{2,1,0:T(8,128)}) async-done(((f32[128,256]{0,1:T(8,128)}, f32[4,128,128]{2,1,0:T(8,128)}), (f32[128,256]{0,1:T(8,128)}, f32[4,128,128]{2,1,0:T(8,128)})) %all-reduce.16.cloned.1.call-update) | async-done | bytes 393232 | tf_op jit(solution)/shard_map/psum | solution.py:38
  68.5 1.2 fusion.39
  69.7 1.1 fusion.38
  70.8 1.1 fusion.37
  71.9 1.1 fusion.36
  74.0 1.3 fusion.14
  75.4 2.9 %convolution_subtract_fusion.3 = f32[128,2048]{1,0:T(8,128)S(1)} fusion(f32[128,2048]{1,0:T(8,128)} %bitcast.2, f32[128,256]{1,0:T(8,128)S(1)} %fusion.14, f32[128,2048]{1,0:T(8,128)S(1)} %copy-done.3, f32[128,2048]{1,0:T(8,128)} %get-tuple-element.14), kind=kOutput, calls=%fused_computation.7 | convolution fusion | flops 806092800 | bytes 4325376 | tf_op jit(solution)/shard_map/dot_general | solution.py:40
  79.3 2.9 %fusion.5 = f32[128,256]{1,0:T(8,128)} fusion(f32[128,2048]{1,0:T(8,128)S(1)} %convolution_subtract_fusion.3, f32[128,2048]{1,0:T(8,128)S(1)} %copy-done.1, f32[128,2048]{1,0:T(8,128)S(1)} %copy-done.2), kind=kOutput, calls=%fused_computation.14 | convolution fusion | flops 805830656 | bytes 3276800 | tf_op jit(solution)/shard_map/dot_general | solution.py:38
  82.4 1.7 convolution_negate_fusion.2
  84.1 32.7 %all-reduce.10.cloned.1.call-done = f32[128,256]{1,0:T(8,128)} async-done(((f32[128,256]{1,0:T(8,128)}), f32[128,256]{1,0:T(8,128)}) %all-reduce.10.cloned.1.call-update) | async-done | bytes 131088 | tf_op jit(solution)/shard_map/psum | solution.py:38
  116.7 1.4 fusion.12
  118.1 3.2 %convolution_subtract_fusion.2 = f32[128,2048]{1,0:T(8,128)S(1)} fusion(f32[128,2048]{1,0:T(8,128)} %copy-done.5, f32[128,256]{1,0:T(8,128)S(1)} %fusion.12, f32[128,2048]{1,0:T(8,128)} %get-tuple-element.10, f32[128,2048]{1,0:T(8,128)} %get-tuple-element.11), kind=kOutput, calls=%fused_computation.6 | convolution fusion | flops 806092800 | bytes 4325376 | tf_op jit(solution)/shard_map/dot_general | solution.py:40
  122.3 2.9 %fusion.4 = f32[128,256]{1,0:T(8,128)} fusion(f32[128,2048]{1,0:T(8,128)S(1)} %convolution_subtract_fusion.2, f32[128,2048]{1,0:T(8,128)S(1)} %get-tuple-element.8, f32[128,2048]{1,0:T(8,128)S(1)} %copy-done), kind=kOutput, calls=%fused_computation.13 | convolution fusion | flops 805830656 | bytes 3276800 | tf_op jit(solution)/shard_map/dot_general | solution.py:38
  125.2 1.7 convolution_negate_fusion.1
  126.9 32.7 %all-reduce.12.cloned.1.call-done = f32[128,256]{1,0:T(8,128)} async-done(((f32[128,256]{1,0:T(8,128)}), f32[128,256]{1,0:T(8,128)}) %all-reduce.12.cloned.1.call-update) | async-done | bytes 131088 | tf_op jit(solution)/shard_map/psum | solution.py:38
  159.7 1.3 fusion.10
  161.0 2.8 %convolution_subtract_fusion.1 = f32[128,2048]{1,0:T(8,128)S(1)} fusion(f32[128,2048]{1,0:T(8,128)} %copy-done.6, f32[128,256]{1,0:T(8,128)S(1)} %fusion.10, f32[128,2048]{1,0:T(8,128)S(1)} %get-tuple-element.8, f32[128,2048]{1,0:T(8,128)} %get-tuple-element.9), kind=kOutput, calls=%fused_computation.5 | convolution fusion | flops 806092800 | bytes 4325376 | tf_op jit(solution)/shard_map/dot_general | solution.py:40
  164.7 2.9 %fusion.3 = f32[128,256]{1,0:T(8,128)} fusion(f32[128,2048]{1,0:T(8,128)S(1)} %convolution_subtract_fusion.1, f32[128,2048]{1,0:T(8,128)S(1)} %get-tuple-element.12, f32[128,2048]{1,0:T(8,128)S(1)} %get-tuple-element.7), kind=kOutput, calls=%fused_computation.12 | convolution fusion | flops 805830656 | bytes 3276800 | tf_op jit(solution)/shard_map/dot_general | solution.py:38
  167.6 1.0 convolution_negate_fusion
  168.7 33.4 %all-reduce.14.cloned.1.call-done = f32[128,256]{1,0:T(8,128)} async-done(((f32[128,256]{1,0:T(8,128)}), f32[128,256]{1,0:T(8,128)}) %all-reduce.14.cloned.1.call-update) | async-done | bytes 131088 | tf_op jit(solution)/shard_map/psum | solution.py:38
  202.1 1.3 fusion.8
  203.4 3.4 %convolution_subtract_fusion = f32[128,2048]{1,0:T(8,128)} fusion(f32[128,2048]{1,0:T(8,128)} %copy-done.4, f32[128,256]{1,0:T(8,128)S(1)} %fusion.8, f32[128,2048]{1,0:T(8,128)S(1)} %get-tuple-element.12, f32[128,2048]{1,0:T(8,128)S(1)} %get-tuple-element.7), kind=kOutput, calls=%fused_computation.4 | convolution fusion | flops 806092800 | bytes 4325376 | tf_op jit(solution)/shard_map/dot_general | solution.py:40
  206.9 3.8 %all-to-all-start.1 = ((f32[8,16,2048]{2,1,0:T(8,128)}), f32[8,16,2048]{2,1,0:T(8,128)S(1)}, u32[]{:S(2)}, u32[]{:S(2)}) async-start(f32[8,16,2048]{2,1,0:T(8,128)} %bitcast.28), calls=%async_computation.1 | async-start | bytes 2097152 | tf_op jit(solution)/shard_map/all_to_all | solution.py:42
  210.7 15.3 %all-to-all-done.1 = f32[8,16,2048]{2,1,0:T(8,128)S(1)} async-done(((f32[8,16,2048]{2,1,0:T(8,128)}), f32[8,16,2048]{2,1,0:T(8,128)S(1)}, u32[]{:S(2)}, u32[]{:S(2)}) %all-to-all-start.1) | async-done | bytes 1048608 | tf_op jit(solution)/shard_map/all_to_all | solution.py:42
  226.0 1.1 select_bitcast_fusion
  (33 shorter events, 6.0 us)
Async XLA Ops:
  6.5 20.7 %all-to-all-start = ((f32[8,16,2048]{2,1,0:T(8,128)}), f32[8,16,2048]{2,1,0:T(8,128)}, u32[]{:S(2)}, u32[]{:S(2)}) async-start(f32[8,16,2048]{2,1,0:T(8,128)} %bitcast.85), calls=%async_computation | async-start | bytes 2097152 | tf_op jit(solution)/shard_map/all_to_all | solution.py:32
  11.7 56.8 %all-reduce.16.cloned.1.call-start = ((), (), s32[]{:S(2)}) async-start(), calls=%async_computation.5 | async-start | bytes 786432 | tf_op jit(solution)/shard_map/psum | solution.py:38
  31.5 85.2 %all-reduce.10.cloned.1.call-start = ((), (), s32[]{:S(2)}) async-start(), calls=%async_computation.2 | async-start | bytes 262144 | tf_op jit(solution)/shard_map/psum | solution.py:38
  32.7 0.8 copy-start.7
  68.5 6.8 %copy-start.3 = (f32[128,2048]{1,0:T(8,128)S(1)}, f32[128,2048]{1,0:T(8,128)}, u32[]{:S(2)}) copy-start(f32[128,2048]{1,0:T(8,128)} %get-tuple-element.13) | copy-start | bytes 3145732
  75.3 3.9 %copy-start.1 = (f32[128,2048]{1,0:T(8,128)S(1)}, f32[128,2048]{1,0:T(8,128)}, u32[]{:S(2)}) copy-start(f32[128,2048]{1,0:T(8,128)} %get-tuple-element.10) | copy-start | bytes 3145732
  75.3 3.9 %copy-start.2 = (f32[128,2048]{1,0:T(8,128)S(1)}, f32[128,2048]{1,0:T(8,128)}, u32[]{:S(2)}) copy-start(f32[128,2048]{1,0:T(8,128)} %get-tuple-element.11) | copy-start | bytes 3145732
  78.3 1.0 copy-start.5
  82.2 77.5 %all-reduce.12.cloned.1.call-start = ((), (), s32[]{:S(2)}) async-start(), calls=%async_computation.3 | async-start | bytes 262144 | tf_op jit(solution)/shard_map/psum | solution.py:38
  118.1 4.2 %copy-start = (f32[128,2048]{1,0:T(8,128)S(1)}, f32[128,2048]{1,0:T(8,128)}, u32[]{:S(2)}) copy-start(f32[128,2048]{1,0:T(8,128)} %get-tuple-element.9) | copy-start | bytes 3145732
  121.3 1.0 copy-start.6
  121.3 38.3 %copy-start.8 = (f32[128,128]{1,0:T(8,128)S(1)}, f32[128,128]{1,0:T(8,128)}, u32[]{:S(2)}) copy-start(f32[128,128]{1,0:T(8,128)} %get-tuple-element.18) | copy-start | bytes 196612
  125.2 76.9 %all-reduce.14.cloned.1.call-start = ((), (), s32[]{:S(2)}) async-start(), calls=%async_computation.4 | async-start | bytes 262144 | tf_op jit(solution)/shard_map/psum | solution.py:38
  163.8 1.0 copy-start.4
  206.9 3.8 %copy-start.9 = (s32[1,8]{1,0:T(1,128)S(1)}, s32[1,8]{1,0:T(1,128)}, u32[]{:S(2)}) copy-start(s32[1,8]{1,0:T(1,128)} %param.11) | copy-start | bytes 100
  206.9 19.1 %all-to-all-start.1 = ((f32[8,16,2048]{2,1,0:T(8,128)}), f32[8,16,2048]{2,1,0:T(8,128)S(1)}, u32[]{:S(2)}, u32[]{:S(2)}) async-start(f32[8,16,2048]{2,1,0:T(8,128)} %bitcast.28), calls=%async_computation.1 | async-start | bytes 2097152 | tf_op jit(solution)/shard_map/all_to_all | solution.py:42
Sparse Core Ops, SparseCore 0:
  31.7 36.8 all-reduce.15
  82.3 34.4 all-reduce.9
  125.3 34.2 all-reduce.11
  167.8 34.2 all-reduce.13
where the time goes:
time: 234 us
  waiting for transfers between devices  152 us (65%)
  matrix products  45.1 us (19%)
  between operations  14.7 us (6%)
  starting transfers between devices  9.31 us (4%)
  local copies, waits for them, and re-layouts  6.94 us (3%)
  other arithmetic  5.71 us (2%)
    psum x4, waiting for transfers between devices, shards(): lax.psum(jnp.dot(transform_panel, joined.T, precision=high), 'section')  133 us
    all_to_all x1, waiting for transfers between devices, shards(): lax.all_to_all(moved, 'group', split_axis=0, concat_axis=0, tiled=True)  15.3 us
    dot_general x4, matrix products, shards(): jnp.dot(transform_panel, joined.T, precision=high)  12.9 us
    dot_general x4, matrix products, shards(): transform_panel = transform_panel - jnp.dot(scaled, joined, precision=high)  12.3 us
    dot_general x4, matrix products, shards(): jnp.dot(jnp.dot(upper_t, correlation_all[pair], precision=high), lower_t,...  5.47 us
    dot_general x4, matrix products, shards(): scaled = jnp.dot(inner, factor.T, precision=high)  5.29 us
    all_to_all x1, starting transfers between devices, shards(): lax.all_to_all(columns[0], 'group', split_axis=0, concat_axis=0, tiled=True)  5.2 us
  transfers between devices with their start and end apart: 6, of which 6 were waited for; matrix products, arithmetic and copies ran while one was open for 7% of the time, Pallas kernels for 0%

commit v1 on v0

--- a/solution.py
+++ b/solution.py
@@ -35,7 +35,9 @@
     transform_panel = panel
     for pair in reversed(range(count // 2)):
         joined, factor = merged[pair]
-        inner = lax.psum(jnp.dot(transform_panel, joined.T, precision=high), "section")
+        inner = jnp.sum(
+            lax.all_gather(jnp.dot(transform_panel, joined.T, precision=high), "section"), axis=0
+        )
         scaled = jnp.dot(inner, factor.T, precision=high)
         transform_panel = transform_panel - jnp.dot(scaled, joined, precision=high)
     moved = transform_panel.reshape(shape)

time: 234 us -> 194 us (0.83)
  waiting for transfers between devices: 152 us -> 40.1 us
  blocking collectives: 0 us -> 64.5 us
  local copies, waits for them, and re-layouts: 6.94 us -> 13.8 us
  other arithmetic: 5.71 us -> 9.27 us
  matrix products: 45.1 us -> 41.6 us
    psum x4 -> x1, waiting for transfers between devices: 133 us -> 24.8 us  [shards(): correlation_all = lax.psum(local_correlation, 'section')]
    all_gather x0 -> x4, blocking collectives: none -> 64.5 us  [shards(): lax.all_gather(jnp.dot(transform_panel, joined.T, precision=high), 'secti...]
    reduce_sum x0 -> x4, other arithmetic: none -> 4.61 us  [shards(): jnp.sum(lax.all_gather(jnp.dot(transform_panel, joined.T, precision=high)...]
    all_to_all x1, waiting for transfers between devices: 3.61 us -> 0.01 us  [shards(): lax.all_to_all(columns[0], 'group', split_axis=0, concat_axis=0, tiled=True)]
    squeeze x1, local copies, waits for them, and re-layouts: 2.46 us -> 6.05 us  [shards(): basis_all[2 * pair]]
    dot_general x4, matrix products: 12.9 us -> 10.3 us  [shards(): jnp.dot(transform_panel, joined.T, precision=high)]
    unnamed x20 -> x24, local copies, waits for them, and re-layouts: 3.74 us -> 5.01 us
  transfers between devices with their start and end apart: 6 -> 3, of which waited for: 6 -> 2; matrix products, arithmetic and copies ran while one was open for 7% -> 9% of each run, Pallas kernels for 0% -> 0%
where the time goes in v1:
time: 194 us; the launch traced here: 193 us
  blocking collectives  64.5 us (33%)
  matrix products  41.6 us (21%)
  waiting for transfers between devices  40.1 us (21%)
  between operations  15 us (8%)
  local copies, waits for them, and re-layouts  13.8 us (7%)
  other arithmetic  9.27 us (5%)
  starting transfers between devices  8.9 us (5%)
    all_gather x4, blocking collectives, shards(): lax.all_gather(jnp.dot(transform_panel, joined.T, precision=high), 'secti...  64.5 us
    psum x1, waiting for transfers between devices, shards(): correlation_all = lax.psum(local_correlation, 'section')  24.8 us
    all_to_all x1, waiting for transfers between devices, shards(): lax.all_to_all(moved, 'group', split_axis=0, concat_axis=0, tiled=True)  15.2 us
    dot_general x4, matrix products, shards(): transform_panel = transform_panel - jnp.dot(scaled, joined, precision=high)  11.4 us
    dot_general x4, matrix products, shards(): jnp.dot(transform_panel, joined.T, precision=high)  10.3 us
    dot_general x4, matrix products, shards(): jnp.dot(jnp.dot(upper_t, correlation_all[pair], precision=high), lower_t,...  6.68 us
    squeeze x1, local copies, waits for them, and re-layouts, shards(): basis_all[2 * pair]  6.05 us
    all_to_all x1, starting transfers between devices, shards(): lax.all_to_all(columns[0], 'group', split_axis=0, concat_axis=0, tiled=True)  5.21 us
  transfers between devices with their start and end apart: 3, of which 2 were waited for; matrix products, arithmetic and copies ran while one was open for 9% of the time, Pallas kernels for 0%

profile of v1, /device:TPU:0, one launch (start us, length us, event | category | flops | bytes accessed | tf_op | source)
XLA Modules:
  0.0 193.2 jit_solution(15461055781918794026)
XLA Ops:
  7.2 3.4 %convert_multiply_fusion = f32[8,128,2048]{2,1,0:T(8,128)S(1)} fusion(bf16[1,8,128,2048]{3,2,1,0:T(8,128)(2,1)} %param.7, f32[2048]{0:T(1024)S(1)} %fusion.40), kind=kLoop, calls=%fused_computation | loop fusion | flops 4194304 | bytes 12591104 | tf_op jit(solution)/shard_map/mul | solution.py:14
  10.6 3.2 %copy-done = f32[8,128,2048]{2,1,0:T(8,128)} copy-done((f32[8,128,2048]{2,1,0:T(8,128)}, f32[8,128,2048]{2,1,0:T(8,128)S(1)}, u32[]{:S(2)}) %copy-start) | copy-done | bytes 8388632
  13.8 4.7 %fusion = f32[4,128,128]{2,1,0:T(8,128)} fusion(f32[8,128,2048]{2,1,0:T(8,128)S(1)} %convert_multiply_fusion), kind=kOutput, calls=%fused_computation.1 | convolution fusion | flops 1610612736 | bytes 8650752 | tf_op jit(solution)/shard_map/jar,jbr->jab/dot_general | solution.py:18
  18.5 5.2 %all-to-all-start = ((f32[8,16,2048]{2,1,0:T(8,128)}), f32[8,16,2048]{2,1,0:T(8,128)}, u32[]{:S(2)}, u32[]{:S(2)}) async-start(f32[8,16,2048]{2,1,0:T(8,128)} %bitcast.1), calls=%async_computation | async-start | bytes 2097152 | tf_op jit(solution)/shard_map/all_to_all | solution.py:32
  23.7 6.1 %slice_bitcast_fusion.1 = (f32[128,2048]{1,0:T(8,128)S(1)}, f32[128,2048]{1,0:T(8,128)S(1)}, f32[128,2048]{1,0:T(8,128)}, f32[128,2048]{1,0:T(8,128)}, f32[128,2...) fusion(f32[8,128,2048]{2,1,0:T(8,128)} %copy-done), kind=kLoop, calls=%fused_computation.22 | loop fusion | bytes 16777216 | tf_op jit(solution)/shard_map/squeeze | solution.py:30
  32.1 24.8 %all-reduce.6.cloned.1.call-done = f32[4,128,128]{2,1,0:T(8,128)} async-done(((f32[4,128,128]{2,1,0:T(8,128)}), f32[4,128,128]{2,1,0:T(8,128)}) %all-reduce.6.cloned.1.call-update) | async-done | bytes 262160 | tf_op jit(solution)/shard_map/psum | solution.py:19
  58.0 1.7 convolution_negate_fusion.3
  60.7 1.7 convolution_negate_fusion.2
  63.5 1.7 convolution_negate_fusion.1
  66.2 1.7 convolution_negate_fusion
  67.9 3.6 %fusion.7 = f32[128,256]{0,1:T(8,128)S(1)} fusion(f32[128,2048]{1,0:T(8,128)} %bitcast.2, f32[128,2048]{1,0:T(8,128)} %get-tuple-element.11, f32[128,2048]{1,0:T(8,128)} %get-tuple-element.12), kind=kOutput, calls=%fused_computation.16 | convolution fusion | flops 805830656 | bytes 3276800 | tf_op jit(solution)/shard_map/dot_general | solution.py:39
  71.6 16.9 %all-gather = f32[512,256]{0,1:T(8,128)} all-gather(f32[128,256]{0,1:T(8,128)S(1)} %fusion.7), channel_id=2, replica_groups=mesh['group'=8,'section'=4] {'section'}, dimensions={0}, use_global_device_ids=true | all-gather | bytes 655360 | tf_op jit(solution)/shard_map/all_gather | solution.py:39
  88.5 2.0 %reshape.46 = f32[4,128,256]{1,0,2:T(4,128)} reshape(f32[512,256]{0,1:T(8,128)} %all-gather) | data formatting | bytes 1048576 | tf_op jit(solution)/shard_map/all_gather | solution.py:39
  90.5 1.4 reduce_sum.36
  91.9 1.3 fusion.14
  93.2 3.2 %convolution_subtract_fusion.3 = f32[128,2048]{1,0:T(8,128)S(1)} fusion(f32[128,2048]{1,0:T(8,128)} %bitcast.2, f32[128,256]{1,0:T(8,128)S(1)} %fusion.14, f32[128,2048]{1,0:T(8,128)} %get-tuple-element.11, f32[128,2048]{1,0:T(8,128)} %get-tuple-element.12), kind=kOutput, calls=%fused_computation.7 | convolution fusion | flops 806092800 | bytes 4325376 | tf_op jit(solution)/shard_map/dot_general | solution.py:42
  96.5 2.2 %fusion.5 = f32[128,256]{1,0:T(8,128)S(1)} fusion(f32[128,2048]{1,0:T(8,128)S(1)} %convolution_subtract_fusion.3, f32[128,2048]{1,0:T(8,128)S(1)} %copy-done.2, f32[128,2048]{1,0:T(8,128)S(1)} %copy-done.3), kind=kOutput, calls=%fused_computation.14 | convolution fusion | flops 805830656 | bytes 3276800 | tf_op jit(solution)/shard_map/dot_general | solution.py:39
  98.7 16.6 %all-gather.1 = f32[512,256]{1,0:T(8,128)} all-gather(f32[128,256]{1,0:T(8,128)S(1)} %fusion.5), channel_id=3, replica_groups=mesh['group'=8,'section'=4] {'section'}, dimensions={0}, use_global_device_ids=true | all-gather | bytes 655360 | tf_op jit(solution)/shard_map/all_gather | solution.py:39
  115.3 1.1 reduce_sum.37
  116.4 1.3 fusion.12
  117.7 3.2 %convolution_subtract_fusion.2 = f32[128,2048]{1,0:T(8,128)S(1)} fusion(f32[128,2048]{1,0:T(8,128)} %copy-done.6, f32[128,256]{1,0:T(8,128)S(1)} %fusion.12, f32[128,2048]{1,0:T(8,128)} %get-tuple-element.8, f32[128,2048]{1,0:T(8,128)} %get-tuple-element.9), kind=kOutput, calls=%fused_computation.6 | convolution fusion | flops 806092800 | bytes 4325376 | tf_op jit(solution)/shard_map/dot_general | solution.py:42
  120.9 2.2 %fusion.4 = f32[128,256]{1,0:T(8,128)S(1)} fusion(f32[128,2048]{1,0:T(8,128)S(1)} %convolution_subtract_fusion.2, f32[128,2048]{1,0:T(8,128)S(1)} %get-tuple-element.6, f32[128,2048]{1,0:T(8,128)S(1)} %copy-done.1), kind=kOutput, calls=%fused_computation.13 | convolution fusion | flops 805830656 | bytes 3276800 | tf_op jit(solution)/shard_map/dot_general | solution.py:39
  123.2 15.4 %all-gather.2 = f32[512,256]{1,0:T(8,128)} all-gather(f32[128,256]{1,0:T(8,128)S(1)} %fusion.4), channel_id=4, replica_groups=mesh['group'=8,'section'=4] {'section'}, dimensions={0}, use_global_device_ids=true | all-gather | bytes 655360 | tf_op jit(solution)/shard_map/all_gather | solution.py:39
  138.6 1.1 reduce_sum.38
  139.7 1.2 fusion.10
  140.9 2.8 %convolution_subtract_fusion.1 = f32[128,2048]{1,0:T(8,128)S(1)} fusion(f32[128,2048]{1,0:T(8,128)} %copy-done.7, f32[128,256]{1,0:T(8,128)S(1)} %fusion.10, f32[128,2048]{1,0:T(8,128)S(1)} %get-tuple-element.6, f32[128,2048]{1,0:T(8,128)} %get-tuple-element.7), kind=kOutput, calls=%fused_computation.5 | convolution fusion | flops 806092800 | bytes 4325376 | tf_op jit(solution)/shard_map/dot_general | solution.py:42
  144.7 2.2 %fusion.3 = f32[128,256]{1,0:T(8,128)S(1)} fusion(f32[128,2048]{1,0:T(8,128)S(1)} %convolution_subtract_fusion.1, f32[128,2048]{1,0:T(8,128)S(1)} %get-tuple-element.10, f32[128,2048]{1,0:T(8,128)S(1)} %get-tuple-element.5), kind=kOutput, calls=%fused_computation.12 | convolution fusion | flops 805830656 | bytes 3276800 | tf_op jit(solution)/shard_map/dot_general | solution.py:39
  146.9 15.5 %all-gather.3 = f32[512,256]{1,0:T(8,128)} all-gather(f32[128,256]{1,0:T(8,128)S(1)} %fusion.3), channel_id=5, replica_groups=mesh['group'=8,'section'=4] {'section'}, dimensions={0}, use_global_device_ids=true | all-gather | bytes 655360 | tf_op jit(solution)/shard_map/all_gather | solution.py:39
  164.0 2.2 %convolution_subtract_fusion = f32[128,2048]{1,0:T(8,128)} fusion(f32[128,2048]{1,0:T(8,128)S(1)} %copy-done.5, f32[128,256]{1,0:T(8,128)S(1)} %fusion.8, f32[128,2048]{1,0:T(8,128)S(1)} %get-tuple-element.10, f32[128,2048]{1,0:T(8,128)S(1)} %get-tuple-element.5), kind=kOutput, calls=%fused_computation.4 | convolution fusion | flops 806092800 | bytes 4325376 | tf_op jit(solution)/shard_map/dot_general | solution.py:42
  166.2 3.7 %all-to-all-start.1 = ((f32[8,16,2048]{2,1,0:T(8,128)}), f32[8,16,2048]{2,1,0:T(8,128)S(1)}, u32[]{:S(2)}, u32[]{:S(2)}) async-start(f32[8,16,2048]{2,1,0:T(8,128)} %bitcast.90), calls=%async_computation.1 | async-start | bytes 2097152 | tf_op jit(solution)/shard_map/all_to_all | solution.py:44
  170.0 15.2 %all-to-all-done.1 = f32[8,16,2048]{2,1,0:T(8,128)S(1)} async-done(((f32[8,16,2048]{2,1,0:T(8,128)}), f32[8,16,2048]{2,1,0:T(8,128)S(1)}, u32[]{:S(2)}, u32[]{:S(2)}) %all-to-all-start.1) | async-done | bytes 1048608 | tf_op jit(solution)/shard_map/all_to_all | solution.py:44
  185.2 1.1 select_bitcast_fusion
  (37 shorter events, 8.5 us)
Async XLA Ops:
  6.5 50.4 %all-reduce.6.cloned.1.call-start = ((), (), s32[]{:S(2)}) async-start(), calls=%async_computation.2 | async-start | bytes 524288 | tf_op jit(solution)/shard_map/psum | solution.py:19
  10.6 3.2 %copy-start = (f32[8,128,2048]{2,1,0:T(8,128)}, f32[8,128,2048]{2,1,0:T(8,128)S(1)}, u32[]{:S(2)}) copy-start(f32[8,128,2048]{2,1,0:T(8,128)S(1)} %convert_multiply_fusion) | copy-start | bytes 25165828
  18.5 49.4 %all-to-all-start = ((f32[8,16,2048]{2,1,0:T(8,128)}), f32[8,16,2048]{2,1,0:T(8,128)}, u32[]{:S(2)}, u32[]{:S(2)}) async-start(f32[8,16,2048]{2,1,0:T(8,128)} %bitcast.1), calls=%async_computation | async-start | bytes 2097152 | tf_op jit(solution)/shard_map/all_to_all | solution.py:32
  23.7 6.7 %copy-start.9 = (f32[1,8,128,128]{3,2,1,0:T(8,128)S(1)}, f32[1,8,128,128]{3,2,1,0:T(8,128)}, u32[]{:S(2)}) copy-start(f32[1,8,128,128]{3,2,1,0:T(8,128)} %param.8) | copy-start | bytes 1572868
  30.5 0.8 copy-start.8
  93.2 3.3 %copy-start.2 = (f32[128,2048]{1,0:T(8,128)S(1)}, f32[128,2048]{1,0:T(8,128)}, u32[]{:S(2)}) copy-start(f32[128,2048]{1,0:T(8,128)} %get-tuple-element.8) | copy-start | bytes 3145732
  93.2 3.3 %copy-start.3 = (f32[128,2048]{1,0:T(8,128)S(1)}, f32[128,2048]{1,0:T(8,128)}, u32[]{:S(2)}) copy-start(f32[128,2048]{1,0:T(8,128)} %get-tuple-element.9) | copy-start | bytes 3145732
  96.4 2.3 %copy-start.6 = (f32[128,2048]{1,0:T(8,128)}, f32[128,2048]{1,0:T(8,128)S(1)}, u32[]{:S(2)}) copy-start(f32[128,2048]{1,0:T(8,128)S(1)} %convolution_subtract_fusion.3) | copy-start | bytes 3145732
  117.7 3.2 %copy-start.1 = (f32[128,2048]{1,0:T(8,128)S(1)}, f32[128,2048]{1,0:T(8,128)}, u32[]{:S(2)}) copy-start(f32[128,2048]{1,0:T(8,128)} %get-tuple-element.7) | copy-start | bytes 3145732
  120.9 2.2 %copy-start.7 = (f32[128,2048]{1,0:T(8,128)}, f32[128,2048]{1,0:T(8,128)S(1)}, u32[]{:S(2)}) copy-start(f32[128,2048]{1,0:T(8,128)S(1)} %convolution_subtract_fusion.2) | copy-start | bytes 3145732
  143.7 1.0 copy-start.4
  144.7 18.9 %copy-start.10 = (f32[128,128]{1,0:T(8,128)S(1)}, f32[128,128]{1,0:T(8,128)}, u32[]{:S(2)}) copy-start(f32[128,128]{1,0:T(8,128)} %convolution_negate_fusion) | copy-start | bytes 196612
  146.9 17.1 %copy-start.5 = (f32[128,2048]{1,0:T(8,128)S(1)}, f32[128,2048]{1,0:T(8,128)}, u32[]{:S(2)}) copy-start(f32[128,2048]{1,0:T(8,128)} %copy-done.4) | copy-start | bytes 3145732
  166.2 3.7 %copy-start.11 = (s32[1,8]{1,0:T(1,128)S(1)}, s32[1,8]{1,0:T(1,128)}, u32[]{:S(2)}) copy-start(s32[1,8]{1,0:T(1,128)} %param.11) | copy-start | bytes 100
  166.2 19.0 %all-to-all-start.1 = ((f32[8,16,2048]{2,1,0:T(8,128)}), f32[8,16,2048]{2,1,0:T(8,128)S(1)}, u32[]{:S(2)}, u32[]{:S(2)}) async-start(f32[8,16,2048]{2,1,0:T(8,128)} %bitcast.90), calls=%async_computation.1 | async-start | bytes 2097152 | tf_op jit(solution)/shard_map/all_to_all | solution.py:44
Sparse Core Ops, SparseCore 0:
  18.6 38.2 all-reduce.5
